TPU v7x, 256 devices: a whole 4x4x8 slice. The times are simulated.
256 devices in a mesh: intv: 1, node: 16 (over y, x), row: 16 (over z, core).
Axes of the slice: x: 4, y: 4, z: 8, core: 2. Of those that a mesh axis runs over, the one named last changes fastest.
Arguments:
- inv_factors: float32 [16, 16, 2, 512, 512], P(('intv', 'node'), 'row'), may hold values from -0.48535534 to 0.48535534, as said below
- coupling: float32 [16, 512, 512], P('row'), may hold values from -0.5 to 0.5
- vectors: float32 [16, 512, 64], P('row'), may hold values from -6 to 6
Outputs:
- moments: float32 [16, 512, 256], P(('intv', 'row'), 'node')
- gram: float32 [256, 256], P('intv')
Inputs may be any that keep to these rules, and one draw needn't show every extreme that they name: `inv_factors`: each [j, k] entry holds the real part then the imaginary part of a full 512 x 512 inverse factor.
All inputs are finite; a program needn't handle non-finite values.
Results may differ from a plain program's by a relative error of at most 0.0003.
Values sent between devices are 32-bit elements; how exact they have to be, the bound alone decides.
A program may use at most 64 MiB of HBM per device.

v0:
```python
import math

import jax
import jax.numpy as jnp
from jax import lax
from jax.sharding import PartitionSpec as P

MOM = 2


HIGH = lax.Precision.HIGHEST


def shifted(value, axis, steps):
    count = lax.axis_size(axis)
    initial, last = (max(0, -steps), min(count, count - steps))
    return lax.ppermute(value, axis, [(source, source + steps) for source in range(initial, last)])


def total_of_pieces(x, axis):
    return lax.all_gather(x, axis).sum(0)


def complex_product(factor, block):
    half = block.shape[2] // 2
    real_side = jnp.einsum("qij,qjc->qic", factor[:, 0], block, precision=HIGH)
    imag_side = jnp.einsum("qij,qjc->qic", factor[:, 1], block, precision=HIGH)
    return jnp.concatenate(
        [
            real_side[..., :half] - imag_side[..., half:],
            real_side[..., half:] + imag_side[..., :half],
        ],
        axis=2,
    )


def shards(inv_factors, coupling, vectors):
    node_local = inv_factors.shape[0]
    block_local = inv_factors.shape[1]
    block_size = inv_factors.shape[3]
    width = vectors.shape[2]
    row_devices = lax.axis_size("row")
    node_devices = lax.axis_size("node")
    filler = jnp.zeros((block_size, width), jnp.float32)
    starts = [jnp.concatenate([vectors[0], filler], axis=1)]
    empty = jnp.zeros((node_local, block_size, 2 * width), jnp.float32)

    def sweep_forward(incoming):
        carry = incoming
        upper = complex_product(inv_factors[:, 0], starts[0] + carry)
        uppers = [upper]
        carry = jnp.einsum("ji,qjc->qic", coupling[0], upper, precision=HIGH)
        return (uppers, carry)

    carry = empty
    for turn in range(row_devices - 1):
        uppers, leaving = sweep_forward(carry)
        carry = shifted(leaving, "row", 1)
    uppers, leaving = sweep_forward(carry)

    def sweep_backward(following):
        solved = [None] * block_local
        coupled = jnp.einsum("ij,qjc->qic", coupling[0], following, precision=HIGH)
        current = uppers[0] + complex_product(inv_factors[:, 0], coupled)
        solved[0] = current
        return solved

    following = empty
    for turn in range(row_devices - 1):
        solved = sweep_backward(following)
        following = shifted(solved[0], "row", -1)
    solved = sweep_backward(following)
    solutions = jnp.stack(solved, axis=1)
    node_total = node_local * node_devices
    nodes_index = (lax.axis_index("node") * node_local + lax.iota(jnp.int32, node_local)).astype(
        jnp.float32
    )
    theta = 2.0 * math.pi * (nodes_index + 0.5) / node_total
    real_sol = solutions[..., :width]
    imag_sol = solutions[..., width:]
    pieces = []
    for order in range(MOM):
        w_real = jnp.cos((order + 1) * theta) / node_total
        w_imag = jnp.sin((order + 1) * theta) / node_total
        pieces.append(
            jnp.einsum("q,qbrc->brc", w_real, real_sol)
            - jnp.einsum("q,qbrc->brc", w_imag, imag_sol)
        )
        pieces.append(
            jnp.einsum("q,qbrc->brc", w_real, imag_sol)
            + jnp.einsum("q,qbrc->brc", w_imag, real_sol)
        )
    terms = jnp.concatenate(pieces, axis=-1)
    columns = terms.shape[2]
    share_rows = block_size // node_devices
    scale = node_total / (block_local * row_devices * block_size)
    summed = total_of_pieces(terms, "node")
    shares = lax.dynamic_slice_in_dim(summed, lax.axis_index("node") * share_rows, share_rows, 1)
    flat = summed.reshape(block_local * block_size, columns)
    partial_gram = jnp.einsum("rc,rd->cd", flat, flat, precision=HIGH)
    gram = total_of_pieces(partial_gram, "row")
    return (shares, gram * scale)


def solution(mesh):
    return jax.shard_map(
        shards,
        mesh=mesh,
        in_specs=(
            P(("intv", "node"), "row", None, None, None),
            P("row", None, None),
            P("row", None, None),
        ),
        out_specs=(P(("intv", "row"), "node", None), P("intv", None)),
        check_vma=False,
    )
```

profile of v0, /device:TPU:33, one launch (start us, length us, event | category | flops | bytes accessed | tf_op | source)
XLA Modules:
  0.0 518.7 jit_solution(8558489893644354888)
XLA Ops:
  23.8 4.4 collective-permute-start.1
  45.5 4.9 collective-permute-start.3
  88.8 4.6 collective-permute-start.7
  132.1 4.6 collective-permute-start.11
  142.9 5.1 collective-permute-start.12
  154.5 5.6 %collective-permute-start.13 = (f32[1,512,128]{1,2,0:T(8,128)S(1)}, f32[1,512,128]{1,2,0:T(8,128)S(1)}, u32[]{:S(2)}, u32[]{:S(2)}) collective-permute-start(f32[1,512,128]{1,2,0:T(8,128)S(1)} %convolution_bitcast_fusion.37), channel_id=1, source_target_pairs={{0,1},{1,2},{2,3},{3,4},{4,5},{5,6},{6,7},{7,8},{8,9},{9,10},{10,1... | collective-permute-start | bytes 786440 | tf_op jit(solution)/shard_map/ppermute | solution.py:17
  166.5 6.8 %collective-permute-start.14 = (f32[1,512,128]{1,2,0:T(8,128)S(1)}, f32[1,512,128]{1,2,0:T(8,128)S(1)}, u32[]{:S(2)}, u32[]{:S(2)}) collective-permute-start(f32[1,512,128]{1,2,0:T(8,128)S(1)} %convolution_bitcast_fusion.34), channel_id=1, source_target_pairs={{0,1},{1,2},{2,3},{3,4},{4,5},{5,6},{6,7},{7,8},{8,9},{9,10},{10,1... | collective-permute-start | bytes 786440 | tf_op jit(solution)/shard_map/ppermute | solution.py:17
  181.5 6.2 %collective-permute-done.15 = f32[1,512,128]{1,2,0:T(8,128)S(1)} collective-permute-done((f32[1,512,128]{1,2,0:T(8,128)S(1)}, f32[1,512,128]{1,2,0:T(8,128)S(1)}, u32[]{:S(2)}, u32[]{:S(2)}) %collective-permute-start.15) | collective-permute-done | bytes 262176 | tf_op jit(solution)/shard_map/ppermute | solution.py:17
  193.2 8.0 %collective-permute-done.16 = f32[1,512,128]{1,2,0:T(8,128)S(1)} collective-permute-done((f32[1,512,128]{1,2,0:T(8,128)S(1)}, f32[1,512,128]{1,2,0:T(8,128)S(1)}, u32[]{:S(2)}, u32[]{:S(2)}) %collective-permute-start.16) | collective-permute-done | bytes 262176 | tf_op jit(solution)/shard_map/ppermute | solution.py:17
  206.8 6.6 %collective-permute-done.17 = f32[1,512,128]{1,2,0:T(8,128)S(1)} collective-permute-done((f32[1,512,128]{1,2,0:T(8,128)S(1)}, f32[1,512,128]{1,2,0:T(8,128)S(1)}, u32[]{:S(2)}, u32[]{:S(2)}) %collective-permute-start.17) | collective-permute-done | bytes 262176 | tf_op jit(solution)/shard_map/ppermute | solution.py:17
  219.0 6.8 %collective-permute-done.18 = f32[1,512,128]{1,2,0:T(8,128)S(1)} collective-permute-done((f32[1,512,128]{1,2,0:T(8,128)S(1)}, f32[1,512,128]{1,2,0:T(8,128)S(1)}, u32[]{:S(2)}, u32[]{:S(2)}) %collective-permute-start.18) | collective-permute-done | bytes 262176 | tf_op jit(solution)/shard_map/ppermute | solution.py:17
  231.5 7.5 %collective-permute-done.19 = f32[1,512,128]{1,2,0:T(8,128)S(1)} collective-permute-done((f32[1,512,128]{1,2,0:T(8,128)S(1)}, f32[1,512,128]{1,2,0:T(8,128)S(1)}, u32[]{:S(2)}, u32[]{:S(2)}) %collective-permute-start.19) | collective-permute-done | bytes 262176 | tf_op jit(solution)/shard_map/ppermute | solution.py:17
  244.6 7.0 %collective-permute-done.20 = f32[1,512,128]{1,2,0:T(8,128)S(1)} collective-permute-done((f32[1,512,128]{1,2,0:T(8,128)S(1)}, f32[1,512,128]{1,2,0:T(8,128)S(1)}, u32[]{:S(2)}, u32[]{:S(2)}) %collective-permute-start.20) | collective-permute-done | bytes 262176 | tf_op jit(solution)/shard_map/ppermute | solution.py:17
  257.2 7.0 %collective-permute-done.21 = f32[1,512,128]{1,2,0:T(8,128)S(1)} collective-permute-done((f32[1,512,128]{1,2,0:T(8,128)S(1)}, f32[1,512,128]{1,2,0:T(8,128)S(1)}, u32[]{:S(2)}, u32[]{:S(2)}) %collective-permute-start.21) | collective-permute-done | bytes 262176 | tf_op jit(solution)/shard_map/ppermute | solution.py:17
  269.7 7.0 %collective-permute-done.22 = f32[1,512,128]{1,2,0:T(8,128)S(1)} collective-permute-done((f32[1,512,128]{1,2,0:T(8,128)S(1)}, f32[1,512,128]{1,2,0:T(8,128)S(1)}, u32[]{:S(2)}, u32[]{:S(2)}) %collective-permute-start.22) | collective-permute-done | bytes 262176 | tf_op jit(solution)/shard_map/ppermute | solution.py:17
  282.5 6.8 %collective-permute-done.23 = f32[1,512,128]{1,2,0:T(8,128)S(1)} collective-permute-done((f32[1,512,128]{1,2,0:T(8,128)S(1)}, f32[1,512,128]{1,2,0:T(8,128)S(1)}, u32[]{:S(2)}, u32[]{:S(2)}) %collective-permute-start.23) | collective-permute-done | bytes 262176 | tf_op jit(solution)/shard_map/ppermute | solution.py:17
  294.9 7.0 %collective-permute-done.24 = f32[1,512,128]{1,2,0:T(8,128)S(1)} collective-permute-done((f32[1,512,128]{1,2,0:T(8,128)S(1)}, f32[1,512,128]{1,2,0:T(8,128)S(1)}, u32[]{:S(2)}, u32[]{:S(2)}) %collective-permute-start.24) | collective-permute-done | bytes 262176 | tf_op jit(solution)/shard_map/ppermute | solution.py:17
  307.4 7.0 %collective-permute-done.25 = f32[1,512,128]{1,2,0:T(8,128)S(1)} collective-permute-done((f32[1,512,128]{1,2,0:T(8,128)S(1)}, f32[1,512,128]{1,2,0:T(8,128)S(1)}, u32[]{:S(2)}, u32[]{:S(2)}) %collective-permute-start.25) | collective-permute-done | bytes 262176 | tf_op jit(solution)/shard_map/ppermute | solution.py:17
  320.0 7.0 %collective-permute-done.26 = f32[1,512,128]{1,2,0:T(8,128)S(1)} collective-permute-done((f32[1,512,128]{1,2,0:T(8,128)S(1)}, f32[1,512,128]{1,2,0:T(8,128)S(1)}, u32[]{:S(2)}, u32[]{:S(2)}) %collective-permute-start.26) | collective-permute-done | bytes 262176 | tf_op jit(solution)/shard_map/ppermute | solution.py:17
  332.8 6.7 %collective-permute-done.27 = f32[1,512,128]{1,2,0:T(8,128)S(1)} collective-permute-done((f32[1,512,128]{1,2,0:T(8,128)S(1)}, f32[1,512,128]{1,2,0:T(8,128)S(1)}, u32[]{:S(2)}, u32[]{:S(2)}) %collective-permute-start.27) | collective-permute-done | bytes 262176 | tf_op jit(solution)/shard_map/ppermute | solution.py:17
  345.1 7.0 %collective-permute-done.28 = f32[1,512,128]{1,2,0:T(8,128)S(1)} collective-permute-done((f32[1,512,128]{1,2,0:T(8,128)S(1)}, f32[1,512,128]{1,2,0:T(8,128)S(1)}, u32[]{:S(2)}, u32[]{:S(2)}) %collective-permute-start.28) | collective-permute-done | bytes 262176 | tf_op jit(solution)/shard_map/ppermute | solution.py:17
  358.6 7.0 %collective-permute-done.29 = f32[1,512,128]{1,2,0:T(8,128)} collective-permute-done((f32[1,512,128]{1,2,0:T(8,128)}, f32[1,512,128]{1,2,0:T(8,128)}, u32[]{:S(2)}, u32[]{:S(2)}) %collective-permute-start.29) | collective-permute-done | bytes 262176 | tf_op jit(solution)/shard_map/ppermute | solution.py:17
  371.4 89.0 %all-gather.5.cloned.1.call-done = f32[16,512,256]{2,1,0:T(8,128)} async-done(((f32[1,512,256]{2,1,0:T(8,128)}), f32[16,512,256]{2,1,0:T(8,128)}) %all-gather.5.cloned.1.call-update) | async-done | bytes 8388624 | tf_op jit(solution)/shard_map/all_gather | solution.py:21
  466.8 41.4 %all-gather.7.cloned.1.call-done = f32[4096,256]{1,0:T(8,128)} async-done(((f32[256,256]{1,0:T(8,128)}), f32[4096,256]{1,0:T(8,128)}) %all-gather.7.cloned.1.call-update) | async-done | bytes 4194320 | tf_op jit(solution)/shard_map/all_gather | solution.py:21
  (199 shorter events, 231.8 us)
Async XLA Ops:
  7.2 453.3 %all-gather.5.cloned.1.call-start = ((), (), s32[]{:S(2)}) async-start(), calls=%async_computation | async-start | bytes 8912896 | tf_op jit(solution)/shard_map/all_gather | solution.py:21
  23.8 7.7 %collective-permute-start.1 = (f32[1,512,128]{1,2,0:T(8,128)S(1)}, f32[1,512,128]{1,2,0:T(8,128)S(1)}, u32[]{:S(2)}, u32[]{:S(2)}) collective-permute-start(f32[1,512,128]{1,2,0:T(8,128)S(1)} %convolution_bitcast_fusion.73), channel_id=1, source_target_pairs={{0,1},{1,2},{2,3},{3,4},{4,5},{5,6},{6,7},{7,8},{8,9},{9,10},{10,1... | collective-permute-start | bytes 786440 | tf_op jit(solution)/shard_map/ppermute | solution.py:17
  34.6 7.7 %collective-permute-start.2 = (f32[1,512,128]{1,2,0:T(8,128)S(1)}, f32[1,512,128]{1,2,0:T(8,128)S(1)}, u32[]{:S(2)}, u32[]{:S(2)}) collective-permute-start(f32[1,512,128]{1,2,0:T(8,128)S(1)} %convolution_bitcast_fusion.70), channel_id=1, source_target_pairs={{0,1},{1,2},{2,3},{3,4},{4,5},{5,6},{6,7},{7,8},{8,9},{9,10},{10,1... | collective-permute-start | bytes 786440 | tf_op jit(solution)/shard_map/ppermute | solution.py:17
  77.9 7.7 %collective-permute-start.6 = (f32[1,512,128]{1,2,0:T(8,128)S(1)}, f32[1,512,128]{1,2,0:T(8,128)S(1)}, u32[]{:S(2)}, u32[]{:S(2)}) collective-permute-start(f32[1,512,128]{1,2,0:T(8,128)S(1)} %convolution_bitcast_fusion.58), channel_id=1, source_target_pairs={{0,1},{1,2},{2,3},{3,4},{4,5},{5,6},{6,7},{7,8},{8,9},{9,10},{10,1... | collective-permute-start | bytes 786440 | tf_op jit(solution)/shard_map/ppermute | solution.py:17
  110.4 7.7 %collective-permute-start.9 = (f32[1,512,128]{1,2,0:T(8,128)S(1)}, f32[1,512,128]{1,2,0:T(8,128)S(1)}, u32[]{:S(2)}, u32[]{:S(2)}) collective-permute-start(f32[1,512,128]{1,2,0:T(8,128)S(1)} %convolution_bitcast_fusion.49), channel_id=1, source_target_pairs={{0,1},{1,2},{2,3},{3,4},{4,5},{5,6},{6,7},{7,8},{8,9},{9,10},{10,1... | collective-permute-start | bytes 786440 | tf_op jit(solution)/shard_map/ppermute | solution.py:17
  142.9 8.4 %collective-permute-start.12 = (f32[1,512,128]{1,2,0:T(8,128)S(1)}, f32[1,512,128]{1,2,0:T(8,128)S(1)}, u32[]{:S(2)}, u32[]{:S(2)}) collective-permute-start(f32[1,512,128]{1,2,0:T(8,128)S(1)} %convolution_bitcast_fusion.40), channel_id=1, source_target_pairs={{0,1},{1,2},{2,3},{3,4},{4,5},{5,6},{6,7},{7,8},{8,9},{9,10},{10,1... | collective-permute-start | bytes 786440 | tf_op jit(solution)/shard_map/ppermute | solution.py:17
  154.5 8.9 %collective-permute-start.13 = (f32[1,512,128]{1,2,0:T(8,128)S(1)}, f32[1,512,128]{1,2,0:T(8,128)S(1)}, u32[]{:S(2)}, u32[]{:S(2)}) collective-permute-start(f32[1,512,128]{1,2,0:T(8,128)S(1)} %convolution_bitcast_fusion.37), channel_id=1, source_target_pairs={{0,1},{1,2},{2,3},{3,4},{4,5},{5,6},{6,7},{7,8},{8,9},{9,10},{10,1... | collective-permute-start | bytes 786440 | tf_op jit(solution)/shard_map/ppermute | solution.py:17
  166.5 10.1 %collective-permute-start.14 = (f32[1,512,128]{1,2,0:T(8,128)S(1)}, f32[1,512,128]{1,2,0:T(8,128)S(1)}, u32[]{:S(2)}, u32[]{:S(2)}) collective-permute-start(f32[1,512,128]{1,2,0:T(8,128)S(1)} %convolution_bitcast_fusion.34), channel_id=1, source_target_pairs={{0,1},{1,2},{2,3},{3,4},{4,5},{5,6},{6,7},{7,8},{8,9},{9,10},{10,1... | collective-permute-start | bytes 786440 | tf_op jit(solution)/shard_map/ppermute | solution.py:17
  179.1 8.5 %collective-permute-start.15 = (f32[1,512,128]{1,2,0:T(8,128)S(1)}, f32[1,512,128]{1,2,0:T(8,128)S(1)}, u32[]{:S(2)}, u32[]{:S(2)}) collective-permute-start(f32[1,512,128]{1,2,0:T(8,128)S(1)} %maximum_add_fusion.1), channel_id=1, source_target_pairs={{1,0},{2,1},{3,2},{4,3},{5,4},{6,5},{7,6},{8,7},{9,8},{10,9},{11,1... | collective-permute-start | bytes 786440 | tf_op jit(solution)/shard_map/ppermute | solution.py:17
  191.3 9.9 %collective-permute-start.16 = (f32[1,512,128]{1,2,0:T(8,128)S(1)}, f32[1,512,128]{1,2,0:T(8,128)S(1)}, u32[]{:S(2)}, u32[]{:S(2)}) collective-permute-start(f32[1,512,128]{1,2,0:T(8,128)S(1)} %maximum_add_fusion.2), channel_id=1, source_target_pairs={{1,0},{2,1},{3,2},{4,3},{5,4},{6,5},{7,6},{8,7},{9,8},{10,9},{11,1... | collective-permute-start | bytes 786440 | tf_op jit(solution)/shard_map/ppermute | solution.py:17
  204.9 8.5 %collective-permute-start.17 = (f32[1,512,128]{1,2,0:T(8,128)S(1)}, f32[1,512,128]{1,2,0:T(8,128)S(1)}, u32[]{:S(2)}, u32[]{:S(2)}) collective-permute-start(f32[1,512,128]{1,2,0:T(8,128)S(1)} %maximum_add_fusion.3), channel_id=1, source_target_pairs={{1,0},{2,1},{3,2},{4,3},{5,4},{6,5},{7,6},{8,7},{9,8},{10,9},{11,1... | collective-permute-start | bytes 786440 | tf_op jit(solution)/shard_map/ppermute | solution.py:17
  217.1 8.7 %collective-permute-start.18 = (f32[1,512,128]{1,2,0:T(8,128)S(1)}, f32[1,512,128]{1,2,0:T(8,128)S(1)}, u32[]{:S(2)}, u32[]{:S(2)}) collective-permute-start(f32[1,512,128]{1,2,0:T(8,128)S(1)} %maximum_add_fusion.4), channel_id=1, source_target_pairs={{1,0},{2,1},{3,2},{4,3},{5,4},{6,5},{7,6},{8,7},{9,8},{10,9},{11,1... | collective-permute-start | bytes 786440 | tf_op jit(solution)/shard_map/ppermute | solution.py:17
  229.4 9.6 %collective-permute-start.19 = (f32[1,512,128]{1,2,0:T(8,128)S(1)}, f32[1,512,128]{1,2,0:T(8,128)S(1)}, u32[]{:S(2)}, u32[]{:S(2)}) collective-permute-start(f32[1,512,128]{1,2,0:T(8,128)S(1)} %maximum_add_fusion.5), channel_id=1, source_target_pairs={{1,0},{2,1},{3,2},{4,3},{5,4},{6,5},{7,6},{8,7},{9,8},{10,9},{11,1... | collective-permute-start | bytes 786440 | tf_op jit(solution)/shard_map/ppermute | solution.py:17
  242.7 8.9 %collective-permute-start.20 = (f32[1,512,128]{1,2,0:T(8,128)S(1)}, f32[1,512,128]{1,2,0:T(8,128)S(1)}, u32[]{:S(2)}, u32[]{:S(2)}) collective-permute-start(f32[1,512,128]{1,2,0:T(8,128)S(1)} %maximum_add_fusion.6), channel_id=1, source_target_pairs={{1,0},{2,1},{3,2},{4,3},{5,4},{6,5},{7,6},{8,7},{9,8},{10,9},{11,1... | collective-permute-start | bytes 786440 | tf_op jit(solution)/shard_map/ppermute | solution.py:17
  255.3 8.9 %collective-permute-start.21 = (f32[1,512,128]{1,2,0:T(8,128)S(1)}, f32[1,512,128]{1,2,0:T(8,128)S(1)}, u32[]{:S(2)}, u32[]{:S(2)}) collective-permute-start(f32[1,512,128]{1,2,0:T(8,128)S(1)} %maximum_add_fusion.7), channel_id=1, source_target_pairs={{1,0},{2,1},{3,2},{4,3},{5,4},{6,5},{7,6},{8,7},{9,8},{10,9},{11,1... | collective-permute-start | bytes 786440 | tf_op jit(solution)/shard_map/ppermute | solution.py:17
  267.8 8.9 %collective-permute-start.22 = (f32[1,512,128]{1,2,0:T(8,128)S(1)}, f32[1,512,128]{1,2,0:T(8,128)S(1)}, u32[]{:S(2)}, u32[]{:S(2)}) collective-permute-start(f32[1,512,128]{1,2,0:T(8,128)S(1)} %maximum_add_fusion.8), channel_id=1, source_target_pairs={{1,0},{2,1},{3,2},{4,3},{5,4},{6,5},{7,6},{8,7},{9,8},{10,9},{11,1... | collective-permute-start | bytes 786440 | tf_op jit(solution)/shard_map/ppermute | solution.py:17
  280.4 8.9 %collective-permute-start.23 = (f32[1,512,128]{1,2,0:T(8,128)S(1)}, f32[1,512,128]{1,2,0:T(8,128)S(1)}, u32[]{:S(2)}, u32[]{:S(2)}) collective-permute-start(f32[1,512,128]{1,2,0:T(8,128)S(1)} %maximum_add_fusion.9), channel_id=1, source_target_pairs={{1,0},{2,1},{3,2},{4,3},{5,4},{6,5},{7,6},{8,7},{9,8},{10,9},{11,1... | collective-permute-start | bytes 786440 | tf_op jit(solution)/shard_map/ppermute | solution.py:17
  292.9 8.9 %collective-permute-start.24 = (f32[1,512,128]{1,2,0:T(8,128)S(1)}, f32[1,512,128]{1,2,0:T(8,128)S(1)}, u32[]{:S(2)}, u32[]{:S(2)}) collective-permute-start(f32[1,512,128]{1,2,0:T(8,128)S(1)} %maximum_add_fusion.10), channel_id=1, source_target_pairs={{1,0},{2,1},{3,2},{4,3},{5,4},{6,5},{7,6},{8,7},{9,8},{10,9},{11,1... | collective-permute-start | bytes 786440 | tf_op jit(solution)/shard_map/ppermute | solution.py:17
  305.5 8.9 %collective-permute-start.25 = (f32[1,512,128]{1,2,0:T(8,128)S(1)}, f32[1,512,128]{1,2,0:T(8,128)S(1)}, u32[]{:S(2)}, u32[]{:S(2)}) collective-permute-start(f32[1,512,128]{1,2,0:T(8,128)S(1)} %maximum_add_fusion.11), channel_id=1, source_target_pairs={{1,0},{2,1},{3,2},{4,3},{5,4},{6,5},{7,6},{8,7},{9,8},{10,9},{11,1... | collective-permute-start | bytes 786440 | tf_op jit(solution)/shard_map/ppermute | solution.py:17
  318.0 8.9 %collective-permute-start.26 = (f32[1,512,128]{1,2,0:T(8,128)S(1)}, f32[1,512,128]{1,2,0:T(8,128)S(1)}, u32[]{:S(2)}, u32[]{:S(2)}) collective-permute-start(f32[1,512,128]{1,2,0:T(8,128)S(1)} %maximum_add_fusion.12), channel_id=1, source_target_pairs={{1,0},{2,1},{3,2},{4,3},{5,4},{6,5},{7,6},{8,7},{9,8},{10,9},{11,1... | collective-permute-start | bytes 786440 | tf_op jit(solution)/shard_map/ppermute | solution.py:17
  330.6 8.9 %collective-permute-start.27 = (f32[1,512,128]{1,2,0:T(8,128)S(1)}, f32[1,512,128]{1,2,0:T(8,128)S(1)}, u32[]{:S(2)}, u32[]{:S(2)}) collective-permute-start(f32[1,512,128]{1,2,0:T(8,128)S(1)} %maximum_add_fusion.13), channel_id=1, source_target_pairs={{1,0},{2,1},{3,2},{4,3},{5,4},{6,5},{7,6},{8,7},{9,8},{10,9},{11,1... | collective-permute-start | bytes 786440 | tf_op jit(solution)/shard_map/ppermute | solution.py:17
  343.1 8.9 %collective-permute-start.28 = (f32[1,512,128]{1,2,0:T(8,128)S(1)}, f32[1,512,128]{1,2,0:T(8,128)S(1)}, u32[]{:S(2)}, u32[]{:S(2)}) collective-permute-start(f32[1,512,128]{1,2,0:T(8,128)S(1)} %maximum_add_fusion.14), channel_id=1, source_target_pairs={{1,0},{2,1},{3,2},{4,3},{5,4},{6,5},{7,6},{8,7},{9,8},{10,9},{11,1... | collective-permute-start | bytes 786440 | tf_op jit(solution)/shard_map/ppermute | solution.py:17
  356.4 9.2 %collective-permute-start.29 = (f32[1,512,128]{1,2,0:T(8,128)}, f32[1,512,128]{1,2,0:T(8,128)}, u32[]{:S(2)}, u32[]{:S(2)}) collective-permute-start(f32[1,512,128]{1,2,0:T(8,128)} %maximum_add_fusion.15), channel_id=1, source_target_pairs={{1,0},{2,1},{3,2},{4,3},{5,4},{6,5},{7,6},{8,7},{9,8},{10,9},{11,1... | collective-permute-start | bytes 786440 | tf_op jit(solution)/shard_map/ppermute | solution.py:17
  371.4 136.9 %all-gather.7.cloned.1.call-start = ((), (), s32[]{:S(2)}) async-start(), calls=%async_computation.1 | async-start | bytes 4456448 | tf_op jit(solution)/shard_map/all_gather | solution.py:21
  (11 other events, 88.3 us)
Sparse Core Ops, SparseCore 0:
  371.5 88.9 all-gather.4
  466.3 41.9 all-gather.6
where the time goes:
time: 529 us; the launch traced here: 519 us
  waiting for transfers between devices  280 us (53%)
  matrix products  111 us (21%)
  starting transfers between devices  101 us (19%)
  between operations  16.1 us (3%)
  other arithmetic  9.92 us (2%)
    ppermute x30, waiting for transfers between devices, shifted(): lax.ppermute(value, axis, [(source, source + steps) for source in range(i...  149 us
    all_gather x2, waiting for transfers between devices, total_of_pieces(): return lax.all_gather(x, axis).sum(0)  130 us
    ppermute x30, starting transfers between devices, shifted(): lax.ppermute(value, axis, [(source, source + steps) for source in range(i...  101 us
    dot_general x32, matrix products, complex_product(): real_side = jnp.einsum('qij,qjc->qic', factor[:, 0], block, precision=HIGH)  39.2 us
    dot_general x32, matrix products, complex_product(): imag_side = jnp.einsum('qij,qjc->qic', factor[:, 1], block, precision=HIGH)  39.1 us
    dot_general x16, matrix products, sweep_backward(): coupled = jnp.einsum('ij,qjc->qic', coupling[0], following, precision=HIGH)  19.8 us
    dot_general x15, matrix products, sweep_forward(): carry = jnp.einsum('ji,qjc->qic', coupling[0], upper, precision=HIGH)  10.7 us
  transfers between devices with their start and end apart: 32, of which 32 were waited for; matrix products, arithmetic and copies ran while one was open for 1% of the time, Pallas kernels for 0%

commit v1 on v0

v1 whole, which is shorter than its diff:
```python
import math

import jax
import jax.numpy as jnp
from jax import lax
from jax.experimental import pallas as pl
from jax.experimental.pallas import tpu as pltpu
from jax.sharding import PartitionSpec as P

F32 = jnp.float32
BF16 = jnp.bfloat16
MESH = pl.DeviceIdType.MESH

BS = 512
NVEC = 64
NODES = 16
ROWS = 16
SHARE = BS // NODES
COLS = 256
PIECE = COLS // NODES
NCH = 4
HALF = NVEC // NCH
CH = 2 * HALF


def split(x):
    high = x.astype(BF16)
    return high, (x - high.astype(F32)).astype(BF16)


def dot(a, b):
    return jnp.dot(a, b, preferred_element_type=F32)


def dot3(ah, al, bh, bl):
    return dot(ah, bh) + (dot(ah, bl) + dot(al, bh))


def complex_apply(both, wh, wl):
    n = both.shape[0] // 2
    z = dot(both, wh[...])
    z = z[:n] + (z[n:] + dot(both[:n], wl[...]))
    h = n // 2
    return jnp.concatenate([z[:h, :BS] - z[h:, BS:], z[:h, BS:] + z[h:, :BS]], axis=0)


def stacked(x):
    high, low = split(x)
    return jnp.concatenate([high, low], axis=0)


def kernel(inv, coup, vec, mom, gram,
           a_f, c_f, v_f, vt, ath, atl, ch, cl, cth, ctl, mth, mtl, nth, ntl,
           yhl, fr, fs, br, xs, ub, xt, xa, xr, ga, gr, pa, pr, qa, go,
           in_sem, fss, frs, bss, brs, xss, xrs, gss, grs, pss, prs, qss, qrs):
    k = lax.axis_index("row")
    n = lax.axis_index("node")
    last = ROWS - 1

    loads = [
        pltpu.make_async_copy(inv.at[0, 0, 0], a_f.at[0], in_sem.at[0]),
        pltpu.make_async_copy(inv.at[0, 0, 1], a_f.at[1], in_sem.at[1]),
        pltpu.make_async_copy(coup.at[0], c_f, in_sem.at[2]),
        pltpu.make_async_copy(vec.at[0], v_f, in_sem.at[3]),
    ]
    for load in loads:
        load.start()

    barrier = pltpu.get_barrier_semaphore()

    @pl.loop(1, NODES)
    def _(d):
        pl.semaphore_signal(barrier, inc=1, device_id={"node": lax.rem(n + d, NODES)}, device_id_type=MESH)

    @pl.loop(1, ROWS)
    def _(d):
        pl.semaphore_signal(barrier, inc=1, device_id={"row": lax.rem(k + d, ROWS)}, device_id_type=MESH)

    for part in range(2):
        loads[part].wait()
        for b in range(4):
            high, low = split(a_f[part, b * 128:(b + 1) * 128, :].T)
            at = part * BS + b * 128
            ath[:, at:at + 128] = high
            atl[:, at:at + 128] = low
    loads[2].wait()
    for b in range(4):
        rows = slice(b * 128, (b + 1) * 128)
        block = c_f[rows, :]
        high, low = split(block)
        ch[rows, :] = high
        cl[rows, :] = low
        high, low = split(block.T)
        cth[:, rows] = high
        ctl[:, rows] = low

    @pl.loop(0, 4)
    def _(b):
        rows = pl.ds(pl.multiple_of(b * 128, 128), 128)
        for part in range(2):
            cols = slice(part * BS, (part + 1) * BS)
            high, low = split(dot3(ath[rows, cols], atl[rows, cols], ch[...], cl[...]))
            mth[rows, cols] = high
            mtl[rows, cols] = low

    loads[3].wait()
    v_t = v_f[...].T
    for q in range(NCH):
        vt[q] = v_t[q * HALF:(q + 1) * HALF]

    def backward_operator():
        @pl.loop(0, 4)
        def _(b):
            rows = pl.ds(pl.multiple_of(b * 128, 128), 128)
            for part in range(2):
                cols = slice(part * BS, (part + 1) * BS)
                high, low = split(dot3(cth[rows, :], ctl[rows, :], ath[:, cols], atl[:, cols]))
                nth[rows, cols] = high
                ntl[rows, cols] = low

    @pl.when(k >= 2)
    def _():
        backward_operator()

    pl.semaphore_wait(barrier, NODES + ROWS - 2)

    @pl.when(k == 0)
    def _():
        fr[...] = jnp.zeros_like(fr)

    def forward_copy(q):
        return pltpu.make_async_remote_copy(
            src_ref=fs.at[q], dst_ref=fr.at[q], send_sem=fss.at[q], recv_sem=frs.at[q],
            device_id={"row": k + 1}, device_id_type=MESH)

    def backward_copy(q):
        return pltpu.make_async_remote_copy(
            src_ref=xs.at[q], dst_ref=br.at[q], send_sem=bss.at[q], recv_sem=brs.at[q],
            device_id={"row": k - 1}, device_id_type=MESH)

    @pl.loop(0, NCH)
    def _(q):
        @pl.when(k > 0)
        def _():
            forward_copy(q).wait_recv()

        carry = fr[q]
        both = stacked(jnp.concatenate([carry[:HALF] + vt[q], carry[HALF:]], axis=0))
        yhl[q] = both

        @pl.when(k < last)
        def _():
            fs[q] = complex_apply(both, mth, mtl)
            forward_copy(q).start()

        @pl.when(k == last)
        def _():
            xs[q] = complex_apply(both, ath, atl)
            backward_copy(q).start()

    @pl.when(k < 2)
    def _():
        backward_operator()

    @pl.when(k < last)
    def _():
        @pl.loop(0, NCH)
        def _(q):
            ub[q] = complex_apply(yhl[q], ath, atl)

        @pl.loop(0, NCH)
        def _(q):
            backward_copy(q).wait_recv()
            xs[q] = ub[q] + complex_apply(stacked(br[q]), nth, ntl)

            @pl.when(k > 0)
            def _():
                backward_copy(q).start()

    for q in range(NCH):
        x = xs[q]
        xt[q * HALF:(q + 1) * HALF, :] = x[:HALF]
        xt[NVEC + q * HALF:NVEC + (q + 1) * HALF, :] = x[HALF:]
    for b in range(4):
        x = xt[:, b * 128:(b + 1) * 128].T
        for s in range(128 // SHARE):
            xa[b * (128 // SHARE) + s] = x[s * SHARE:(s + 1) * SHARE]
    xr[n] = xa[n]

    def spread(axis, count, me, source, target, send, recv, by_target):
        def copy(d):
            peer = lax.rem(me + d, count)
            return pltpu.make_async_remote_copy(
                src_ref=source.at[peer] if by_target else source, dst_ref=target.at[me],
                send_sem=send.at[d], recv_sem=recv.at[me],
                device_id={axis: peer}, device_id_type=MESH)

        def arrival(d):
            peer = lax.rem(me + d, count)
            return pltpu.make_async_remote_copy(
                src_ref=source.at[peer] if by_target else source, dst_ref=target.at[peer],
                send_sem=send.at[d], recv_sem=recv.at[peer],
                device_id={axis: peer}, device_id_type=MESH)

        @pl.loop(1, count)
        def _(d):
            copy(d).start()

        def finish():
            @pl.loop(1, count)
            def _(d):
                arrival(d).wait_recv()

        def sent():
            @pl.loop(1, count)
            def _(d):
                copy(d).wait_send()

        return finish, sent

    finish, sent_x = spread("node", NODES, n, xa, xr, xss, xrs, True)
    finish()

    parts = []
    lane = lax.broadcasted_iota(jnp.int32, (SHARE, 2 * NVEC), 1)
    for order in (1, 2):
        even = jnp.zeros((SHARE, 2 * NVEC), F32)
        odd = jnp.zeros((SHARE, 2 * NVEC), F32)
        for j in range(NODES):
            theta = 2.0 * math.pi * (j + 0.5) / NODES
            x = xr[j]
            even = even + (math.cos(order * theta) / NODES) * x
            odd = odd + (math.sin(order * theta) / NODES) * x
        odd = pltpu.roll(odd, NVEC, 1)
        parts.append(even + jnp.where(lane < NVEC, -odd, odd))
    f = jnp.concatenate(parts, axis=1)
    mom[...] = f

    fh, fl = split(f)
    th, tl = split(f.T)
    product = dot3(th, tl, fh, fl)
    for j in range(NODES):
        ga[j] = product[j * PIECE:(j + 1) * PIECE]
    gr[n] = ga[n]
    finish, sent_g = spread("node", NODES, n, ga, gr, gss, grs, True)
    finish()
    total = gr[0]
    for j in range(1, NODES):
        total = total + gr[j]
    pa[...] = total
    pr[k] = total
    finish, sent_p = spread("row", ROWS, k, pa, pr, pss, prs, False)
    finish()
    total = pr[0]
    for j in range(1, ROWS):
        total = total + pr[j]
    total = total * (NODES / (ROWS * BS))
    qa[...] = total
    go[n] = total
    finish, sent_q = spread("node", NODES, n, qa, go, qss, qrs, False)
    finish()
    for j in range(NODES):
        gram[j * PIECE:(j + 1) * PIECE, :] = go[j]

    @pl.when(k < last)
    def _():
        @pl.loop(0, NCH)
        def _(q):
            forward_copy(q).wait_send()

    @pl.when(k > 0)
    def _():
        @pl.loop(0, NCH)
        def _(q):
            backward_copy(q).wait_send()

    sent_x()
    sent_g()
    sent_p()
    sent_q()


def shards(inv_factors, coupling, vectors):
    moments, gram = pl.pallas_call(
        kernel,
        out_shape=(
            jax.ShapeDtypeStruct((SHARE, COLS), F32),
            jax.ShapeDtypeStruct((COLS, COLS), F32),
        ),
        in_specs=[pl.BlockSpec(memory_space=pl.ANY)] * 3,
        out_specs=[pl.BlockSpec(memory_space=pltpu.VMEM)] * 2,
        scratch_shapes=[
            pltpu.VMEM((2, BS, BS), F32),
            pltpu.VMEM((BS, BS), F32),
            pltpu.VMEM((BS, NVEC), F32),
            pltpu.VMEM((NCH, HALF, BS), F32),
        ]
        + [pltpu.VMEM((BS, 2 * BS), BF16)] * 2
        + [pltpu.VMEM((BS, BS), BF16)] * 4
        + [pltpu.VMEM((BS, 2 * BS), BF16)] * 4
        + [pltpu.VMEM((NCH, 2 * CH, BS), BF16)]
        + [pltpu.VMEM((NCH, CH, BS), F32)] * 5
        + [
            pltpu.VMEM((2 * NVEC, BS), F32),
            pltpu.VMEM((NODES, SHARE, 2 * NVEC), F32),
            pltpu.VMEM((NODES, SHARE, 2 * NVEC), F32),
            pltpu.VMEM((NODES, PIECE, COLS), F32),
            pltpu.VMEM((NODES, PIECE, COLS), F32),
            pltpu.VMEM((PIECE, COLS), F32),
            pltpu.VMEM((ROWS, PIECE, COLS), F32),
            pltpu.VMEM((PIECE, COLS), F32),
            pltpu.VMEM((NODES, PIECE, COLS), F32),
        ]
        + [pltpu.SemaphoreType.DMA((4,))]
        + [pltpu.SemaphoreType.DMA((NCH,))] * 4
        + [pltpu.SemaphoreType.DMA((16,))] * 8,
        compiler_params=pltpu.CompilerParams(
            collective_id=0, has_side_effects=True, vmem_limit_bytes=56 * 1024 * 1024),
    )(inv_factors, coupling, vectors)
    return moments[None], gram


def solution(mesh):
    return jax.shard_map(
        shards,
        mesh=mesh,
        in_specs=(
            P(("intv", "node"), "row", None, None, None),
            P("row", None, None),
            P("row", None, None),
        ),
        out_specs=(P(("intv", "row"), "node", None), P("intv", None)),
        check_vma=False,
    )
```

time: 529 us -> 115 us (0.22); the launches traced: 519 us -> 114 us
  waiting for transfers between devices: 280 us -> 0 us
  matrix products: 111 us -> 0 us
  Pallas kernels: 0 us -> 109 us
  starting transfers between devices: 101 us -> 0 us
  between operations: 16.1 us -> 0.64 us
  other arithmetic: 9.92 us -> 0 us
    ppermute x30 -> x0, waiting for transfers between devices: 149 us -> none  [shifted(): lax.ppermute(value, axis, [(source, source + steps) for source in range(i...]
    all_gather x2 -> x0, waiting for transfers between devices: 130 us -> none  [total_of_pieces(): return lax.all_gather(x, axis).sum(0)]
    dot_general x96 -> x0, matrix products: 111 us -> none  [the longest x32 39.2 us: complex_product(): real_side = jnp.einsum('qij,qjc->qic', factor[:, 0], block, precision=HIGH)]
    pallas_call x0 -> x1, Pallas kernels: none -> 109 us  [shards(): pl.pallas_call(kernel, out_shape=(jax.ShapeDtypeStruct((SHARE, COLS), F32...]
    ppermute x30 -> x0, starting transfers between devices: 101 us -> none  [shifted(): lax.ppermute(value, axis, [(source, source + steps) for source in range(i...]
  transfers between devices with their start and end apart: 32 -> 0, of which waited for: 32 -> 0; matrix products, arithmetic and copies ran while one was open for 1% -> 0% of each run, Pallas kernels for 0% -> 0%
where the time goes in v1:
time: 115 us; the launch traced here: 114 us
  Pallas kernels  109 us (95%)
  local copies, waits for them, and re-layouts  4.78 us (4%)
    pallas_call x1, Pallas kernels, shards(): pl.pallas_call(kernel, out_shape=(jax.ShapeDtypeStruct((SHARE, COLS), F32...  109 us
    unnamed x3, local copies, waits for them, and re-layouts  4.78 us

profile of v1, /device:TPU:33, one launch (start us, length us, event | category | flops | bytes accessed | tf_op | source)
XLA Modules:
  0.0 114.1 jit_solution(7635762582452885846)
XLA Ops:
  0.6 1.7 %copy.5.vec = f32[1,512,64]{2,1,0:T(8,128)} copy(f32[1,512,64]{1,2,0:T(8,128)} %param.5) | data formatting | bytes 262144 | tf_op args[2]
  2.4 108.7 %shard_map.50 = (f32[32,256]{1,0:T(8,128)}, f32[256,256]{1,0:T(8,128)}) custom-call(f32[1,1,2,512,512]{4,3,2,1,0:T(8,128)} %inv.1, f32[1,512,512]{2,1,0:T(8,128)} %coup.1, f32[1,512,64]{2,1,0:T(8,128)} %copy.5.vec), custom_call_target="tpu_custom_call" | custom-call | tf_op jit(solution)/shard_map/pallas_call | solution.py:284
  111.1 1.4 %copy.8 = f32[1,32,256]{2,1,0:T(8,128)} copy(f32[1,32,256]{2,1,0:T(8,128)} %bitcast.1) | data formatting | bytes 65536
  112.5 1.7 %copy.9 = f32[256,256]{1,0:T(8,128)} copy(f32[256,256]{1,0:T(8,128)} %get-tuple-element.9) | data formatting | bytes 524288

commit v2 on v1

--- a/solution.py
+++ b/solution.py
@@ -18,7 +18,7 @@
 SHARE = BS // NODES
 COLS = 256
 PIECE = COLS // NODES
-NCH = 4
+NCH = 8
 HALF = NVEC // NCH
 CH = 2 * HALF
 
@@ -36,26 +36,41 @@
     return dot(ah, bh) + (dot(ah, bl) + dot(al, bh))
 
 
-def complex_apply(both, wh, wl):
-    n = both.shape[0] // 2
-    z = dot(both, wh[...])
-    z = z[:n] + (z[n:] + dot(both[:n], wl[...]))
-    h = n // 2
-    return jnp.concatenate([z[:h, :BS] - z[h:, BS:], z[:h, BS:] + z[h:, :BS]], axis=0)
-
-
 def stacked(x):
     high, low = split(x)
     return jnp.concatenate([high, low], axis=0)
 
 
+def complex_apply(x, wh, wl, groups=1):
+    n = x.shape[0]
+    high, low = split(x)
+    z = dot(jnp.concatenate([high, low], axis=0), wh[...])
+    z = z[:n] + (z[n:] + dot(high, wl[...]))
+    h = n // groups // 2
+    out = []
+    for g in range(groups):
+        re = slice(2 * g * h, (2 * g + 1) * h)
+        im = slice((2 * g + 1) * h, (2 * g + 2) * h)
+        out.append(z[re, :BS] - z[im, BS:])
+        out.append(z[re, BS:] + z[im, :BS])
+    return jnp.concatenate(out, axis=0)
+
+
+def apply_all(x, wh, wl):
+    return complex_apply(x.reshape(NCH * CH, BS), wh, wl, NCH).reshape(NCH, CH, BS)
+
+
 def kernel(inv, coup, vec, mom, gram,
-           a_f, c_f, v_f, vt, ath, atl, ch, cl, cth, ctl, mth, mtl, nth, ntl,
-           yhl, fr, fs, br, xs, ub, xt, xa, xr, ga, gr, pa, pr, qa, go,
-           in_sem, fss, frs, bss, brs, xss, xrs, gss, grs, pss, prs, qss, qrs):
+           a_f, c_f, v_f, vt, vo, ath, atl, ch, cl, cth, ctl, mth, mtl, nth, ntl, pth, ptl, qth, qtl,
+           snd, rcv, qf, yb, dd, fr, cf, fo, fs, us, uo, es, eo, br, xe, xs,
+           xt, xa, xr, ga, gr, pa, pr, qa, go,
+           in_sem, pss, prs, css, crs, xss, xrs, gss, grs, hss, hrs, qss, qrs):
     k = lax.axis_index("row")
     n = lax.axis_index("node")
-    last = ROWS - 1
+    core = lax.rem(k, 2)
+    z = lax.div(k, 2)
+    top = ROWS // 2 - 1
+    partner = k + 1 - 2 * core
 
     loads = [
         pltpu.make_async_copy(inv.at[0, 0, 0], a_f.at[0], in_sem.at[0]),
@@ -93,89 +108,288 @@
         high, low = split(block.T)
         cth[:, rows] = high
         ctl[:, rows] = low
-
-    @pl.loop(0, 4)
-    def _(b):
-        rows = pl.ds(pl.multiple_of(b * 128, 128), 128)
-        for part in range(2):
-            cols = slice(part * BS, (part + 1) * BS)
-            high, low = split(dot3(ath[rows, cols], atl[rows, cols], ch[...], cl[...]))
-            mth[rows, cols] = high
-            mtl[rows, cols] = low
-
     loads[3].wait()
     v_t = v_f[...].T
     for q in range(NCH):
         vt[q] = v_t[q * HALF:(q + 1) * HALF]
 
-    def backward_operator():
-        @pl.loop(0, 4)
-        def _(b):
-            rows = pl.ds(pl.multiple_of(b * 128, 128), 128)
+    def block_loop(count):
+        def wrap(step):
+            @pl.loop(0, count)
+            def _(b):
+                step(pl.ds(pl.multiple_of(b * (BS // count), BS // count), BS // count))
+        return wrap
+
+    def forward_operator(keep):
+        @block_loop(4)
+        def _(rows):
             for part in range(2):
                 cols = slice(part * BS, (part + 1) * BS)
-                high, low = split(dot3(cth[rows, :], ctl[rows, :], ath[:, cols], atl[:, cols]))
+                value = dot3(ath[rows, cols], atl[rows, cols], ch[...], cl[...])
+                if keep:
+                    snd[rows, cols] = value
+                high, low = split(value)
+                mth[rows, cols] = high
+                mtl[rows, cols] = low
+
+    def backward_operator(keep):
+        @block_loop(4)
+        def _(rows):
+            for part in range(2):
+                cols = slice(part * BS, (part + 1) * BS)
+                value = dot3(cth[rows, :], ctl[rows, :], ath[:, cols], atl[:, cols])
+                if keep:
+                    snd[rows, cols] = value
+                high, low = split(value)
                 nth[rows, cols] = high
                 ntl[rows, cols] = low
 
-    @pl.when(k >= 2)
+    def compose(left, rows, wh, wl):
+        x = jnp.concatenate([left[rows, :BS], left[rows, BS:]], axis=0)
+        out = complex_apply(x, wh, wl)
+        half = out.shape[0] // 2
+        return out[:half], out[half:]
+
+    def store_split(rows, parts, wh, wl):
+        for part, value in enumerate(parts):
+            cols = slice(part * BS, (part + 1) * BS)
+            high, low = split(value)
+            wh[rows, cols] = high
+            wl[rows, cols] = low
+
+    def chunk_copy(kind, source, target, row):
+        def make(q):
+            return pltpu.make_async_remote_copy(
+                src_ref=source.at[q], dst_ref=target.at[q], send_sem=css.at[kind, q], recv_sem=crs.at[kind, q],
+                device_id={"row": row}, device_id_type=MESH)
+        return make
+
+    def whole_copy(kind, source, target):
+        return pltpu.make_async_remote_copy(
+            src_ref=source, dst_ref=target, send_sem=pss.at[kind], recv_sem=prs.at[kind],
+            device_id={"row": partner}, device_id_type=MESH)
+
+    forward = chunk_copy(0, fs, fr, k + 2)
+    relay = chunk_copy(1, fr, cf, partner)
+    inner = chunk_copy(2, fs, fo, partner)
+    upper = chunk_copy(3, us, uo, partner)
+    term = chunk_copy(4, es, eo, partner)
+    backward = chunk_copy(5, xe, br, k - 2)
+    solved = chunk_copy(6, xe, xs, partner)
+    operator = whole_copy(0, snd, rcv)
+    probe = whole_copy(1, vt, vo)
+    second = whole_copy(2, qf, qf)
+
+    def chunks(step):
+        @pl.loop(0, NCH)
+        def _(q):
+            step(q)
+
+    def shifted_by(carry, v):
+        return jnp.concatenate([carry[:HALF] + v, carry[HALF:]], axis=0)
+
+    def enter():
+        pl.semaphore_wait(barrier, NODES + ROWS - 2)
+
+    def real_rows(v):
+        return jnp.concatenate([v, jnp.zeros_like(v)], axis=0)
+
+    def even_forward(first):
+        @chunks
+        def _(q):
+            if first:
+                y = real_rows(vt[q])
+            else:
+                relay(q).wait_recv()
+                y = shifted_by(cf[q], vt[q])
+            yb[q] = y
+            fs[q] = complex_apply(y, mth, mtl)
+            inner(q).start()
+
+    @pl.when(core == 0)
     def _():
-        backward_operator()
-
-    pl.semaphore_wait(barrier, NODES + ROWS - 2)
-
-    @pl.when(k == 0)
+        forward_operator(True)
+        enter()
+        probe.start()
+
+        @pl.when((z > 0) & (z < top))
+        def _():
+            operator.start()
+
+        @pl.when(z == 0)
+        def _():
+            even_forward(True)
+
+        backward_operator(False)
+        operator.wait_recv()
+        probe.wait_recv()
+
+        @pl.when(z < top)
+        def _():
+            @block_loop(8)
+            def _(rows):
+                re, im = compose(rcv, rows, nth, ntl)
+                qf[rows, :BS] = re
+                qf[rows, BS:] = im
+
+        @pl.when(z == top)
+        def _():
+            @block_loop(8)
+            def _(rows):
+                store_split(rows, compose(rcv, rows, nth, ntl), pth, ptl)
+
+            @block_loop(8)
+            def _(rows):
+                re, im = compose(snd, rows, pth, ptl)
+                qf[rows, :BS] = re + (ath[rows, :BS].astype(F32) + atl[rows, :BS].astype(F32))
+                qf[rows, BS:] = im + (ath[rows, BS:].astype(F32) + atl[rows, BS:].astype(F32))
+
+        second.start()
+
+        @pl.when(z == top)
+        def _():
+            @chunks
+            def _(q):
+                es[q] = complex_apply(real_rows(vo[q]), pth, ptl)
+                term(q).start()
+
+        @pl.when(z > 0)
+        def _():
+            even_forward(False)
+
+        @pl.when(z < top)
+        def _():
+            us[...] = apply_all(yb[...], ath, atl)
+
+            @chunks
+            def _(q):
+                upper(q).wait_recv()
+                es[q] = us[q] + complex_apply(uo[q], nth, ntl)
+                term(q).start()
+
+        @chunks
+        def _(q):
+            solved(q).wait_recv()
+
+    def odd_upper():
+        @chunks
+        def _(q):
+            inner(q).wait_recv()
+            yb[q] = shifted_by(fo[q], vt[q])
+
+        us[...] = apply_all(yb[...], ath, atl)
+
+        @chunks
+        def _(q):
+            upper(q).start()
+
+    @pl.when(core == 1)
     def _():
-        fr[...] = jnp.zeros_like(fr)
-
-    def forward_copy(q):
-        return pltpu.make_async_remote_copy(
-            src_ref=fs.at[q], dst_ref=fr.at[q], send_sem=fss.at[q], recv_sem=frs.at[q],
-            device_id={"row": k + 1}, device_id_type=MESH)
-
-    def backward_copy(q):
-        return pltpu.make_async_remote_copy(
-            src_ref=xs.at[q], dst_ref=br.at[q], send_sem=bss.at[q], recv_sem=brs.at[q],
-            device_id={"row": k - 1}, device_id_type=MESH)
-
-    @pl.loop(0, NCH)
-    def _(q):
-        @pl.when(k > 0)
-        def _():
-            forward_copy(q).wait_recv()
-
-        carry = fr[q]
-        both = stacked(jnp.concatenate([carry[:HALF] + vt[q], carry[HALF:]], axis=0))
-        yhl[q] = both
-
-        @pl.when(k < last)
-        def _():
-            fs[q] = complex_apply(both, mth, mtl)
-            forward_copy(q).start()
-
-        @pl.when(k == last)
-        def _():
-            xs[q] = complex_apply(both, ath, atl)
-            backward_copy(q).start()
-
-    @pl.when(k < 2)
-    def _():
-        backward_operator()
-
-    @pl.when(k < last)
-    def _():
-        @pl.loop(0, NCH)
-        def _(q):
-            ub[q] = complex_apply(yhl[q], ath, atl)
-
-        @pl.loop(0, NCH)
-        def _(q):
-            backward_copy(q).wait_recv()
-            xs[q] = ub[q] + complex_apply(stacked(br[q]), nth, ntl)
-
-            @pl.when(k > 0)
-            def _():
-                backward_copy(q).start()
+        @pl.when(z == 0)
+        def _():
+            forward_operator(False)
+            enter()
+            probe.start()
+
+            @chunks
+            def _(q):
+                inner(q).wait_recv()
+                y = shifted_by(fo[q], vt[q])
+                yb[q] = y
+                fs[q] = complex_apply(y, mth, mtl)
+                forward(q).start()
+
+            us[...] = apply_all(yb[...], ath, atl)
+
+            @chunks
+            def _(q):
+                upper(q).start()
+
+            backward_operator(True)
+            operator.start()
+            probe.wait_recv()
+
+        @pl.when((z > 0) & (z < top))
+        def _():
+            backward_operator(True)
+            enter()
+            operator.start()
+            probe.start()
+            forward_operator(False)
+
+            @chunks
+            def _(q):
+                dd[q] = complex_apply(real_rows(vt[q]), mth, mtl)
+
+            operator.wait_recv()
+
+            @block_loop(8)
+            def _(rows):
+                store_split(rows, compose(rcv, rows, mth, mtl), pth, ptl)
+
+            probe.wait_recv()
+
+            @chunks
+            def _(q):
+                forward(q).wait_recv()
+                relay(q).start()
+                fs[q] = dd[q] + complex_apply(shifted_by(fr[q], vo[q]), pth, ptl)
+                forward(q).start()
+
+            odd_upper()
+
+        def take_second(wh, wl):
+            second.wait_recv()
+
+            @block_loop(8)
+            def _(rows):
+                store_split(rows, (qf[rows, :BS], qf[rows, BS:]), wh, wl)
+
+        @pl.when(z == top)
+        def _():
+            @block_loop(8)
+            def _(rows):
+                snd[rows, :] = ath[rows, :].astype(F32) + atl[rows, :].astype(F32)
+
+            enter()
+            operator.start()
+            probe.start()
+            probe.wait_recv()
+            take_second(pth, ptl)
+
+            @chunks
+            def _(q):
+                forward(q).wait_recv()
+                relay(q).start()
+                term(q).wait_recv()
+                xe[q] = eo[q] + complex_apply(shifted_by(fr[q], vo[q]), pth, ptl)
+                backward(q).start()
+                solved(q).start()
+
+            @chunks
+            def _(q):
+                inner(q).wait_recv()
+                yb[q] = shifted_by(fo[q], vt[q])
+
+            xs[...] = apply_all(yb[...], ath, atl)
+
+        @pl.when(z < top)
+        def _():
+            take_second(qth, qtl)
+
+            @chunks
+            def _(q):
+                term(q).wait_recv()
+                backward(q).wait_recv()
+                xe[q] = eo[q] + complex_apply(br[q], qth, qtl)
+
+                @pl.when(z > 0)
+                def _():
+                    backward(q).start()
+
+                solved(q).start()
+
+            xs[...] = us[...] + apply_all(br[...], nth, ntl)
 
     for q in range(NCH):
         x = xs[q]
@@ -249,7 +463,7 @@
         total = total + gr[j]
     pa[...] = total
     pr[k] = total
-    finish, sent_p = spread("row", ROWS, k, pa, pr, pss, prs, False)
+    finish, sent_p = spread("row", ROWS, k, pa, pr, hss, hrs, False)
     finish()
     total = pr[0]
     for j in range(1, ROWS):
@@ -262,17 +476,40 @@
     for j in range(NODES):
         gram[j * PIECE:(j + 1) * PIECE, :] = go[j]
 
-    @pl.when(k < last)
+    probe.wait_send()
+
+    @pl.when((core == 1) | ((z > 0) & (z < top)))
     def _():
-        @pl.loop(0, NCH)
-        def _(q):
-            forward_copy(q).wait_send()
-
-    @pl.when(k > 0)
+        operator.wait_send()
+
+    @pl.when(core == 0)
     def _():
-        @pl.loop(0, NCH)
-        def _(q):
-            backward_copy(q).wait_send()
+        second.wait_send()
+
+        @chunks
+        def _(q):
+            inner(q).wait_send()
+            term(q).wait_send()
+
+    @pl.when(core == 1)
+    def _():
+        @chunks
+        def _(q):
+            solved(q).wait_send()
+
+        @pl.when(z > 0)
+        def _():
+            @chunks
+            def _(q):
+                relay(q).wait_send()
+                backward(q).wait_send()
+
+        @pl.when(z < top)
+        def _():
+            @chunks
+            def _(q):
+                forward(q).wait_send()
+                upper(q).wait_send()
 
     sent_x()
     sent_g()
@@ -281,6 +518,10 @@
 
 
 def shards(inv_factors, coupling, vectors):
+    chunk = pltpu.VMEM((NCH, CH, BS), F32)
+    whole = pltpu.VMEM((BS, 2 * BS), F32)
+    whole_part = pltpu.VMEM((BS, 2 * BS), BF16)
+    square_part = pltpu.VMEM((BS, BS), BF16)
     moments, gram = pl.pallas_call(
         kernel,
         out_shape=(
@@ -294,12 +535,13 @@
             pltpu.VMEM((BS, BS), F32),
             pltpu.VMEM((BS, NVEC), F32),
             pltpu.VMEM((NCH, HALF, BS), F32),
+            pltpu.VMEM((NCH, HALF, BS), F32),
         ]
-        + [pltpu.VMEM((BS, 2 * BS), BF16)] * 2
-        + [pltpu.VMEM((BS, BS), BF16)] * 4
-        + [pltpu.VMEM((BS, 2 * BS), BF16)] * 4
-        + [pltpu.VMEM((NCH, 2 * CH, BS), BF16)]
-        + [pltpu.VMEM((NCH, CH, BS), F32)] * 5
+        + [whole_part] * 2
+        + [square_part] * 4
+        + [whole_part] * 8
+        + [whole] * 3
+        + [chunk] * 13
         + [
             pltpu.VMEM((2 * NVEC, BS), F32),
             pltpu.VMEM((NODES, SHARE, 2 * NVEC), F32),
@@ -312,7 +554,8 @@
             pltpu.VMEM((NODES, PIECE, COLS), F32),
         ]
         + [pltpu.SemaphoreType.DMA((4,))]
-        + [pltpu.SemaphoreType.DMA((NCH,))] * 4
+        + [pltpu.SemaphoreType.DMA((3,))] * 2
+        + [pltpu.SemaphoreType.DMA((7, NCH))] * 2
         + [pltpu.SemaphoreType.DMA((16,))] * 8,
         compiler_params=pltpu.CompilerParams(
             collective_id=0, has_side_effects=True, vmem_limit_bytes=56 * 1024 * 1024),

time: 115 us -> 90.5 us (0.79)
  Pallas kernels: 109 us -> 84.2 us
    pallas_call x1, Pallas kernels: 109 us -> 84.2 us  [shards(): pl.pallas_call(kernel, out_shape=(jax.ShapeDtypeStruct((SHARE, COLS), F32...]
where the time goes in v2:
time: 90.5 us; the launch traced here: 89.6 us
  Pallas kernels  84.2 us (93%)
  local copies, waits for them, and re-layouts  4.78 us (5%)
    pallas_call x1, Pallas kernels, shards(): pl.pallas_call(kernel, out_shape=(jax.ShapeDtypeStruct((SHARE, COLS), F32...  84.2 us
    unnamed x3, local copies, waits for them, and re-layouts  4.78 us

profile of v2, /device:TPU:33, one launch (start us, length us, event | category | flops | bytes accessed | tf_op | source)
XLA Modules:
  0.0 89.6 jit_solution(14940743713031932691)
XLA Ops:
  0.6 1.7 %copy.5.vec = f32[1,512,64]{2,1,0:T(8,128)} copy(f32[1,512,64]{1,2,0:T(8,128)} %param.5) | data formatting | bytes 262144 | tf_op args[2]
  2.4 84.2 %shard_map.50 = (f32[32,256]{1,0:T(8,128)}, f32[256,256]{1,0:T(8,128)}) custom-call(f32[1,1,2,512,512]{4,3,2,1,0:T(8,128)} %inv.1, f32[1,512,512]{2,1,0:T(8,128)} %coup.1, f32[1,512,64]{2,1,0:T(8,128)} %copy.5.vec), custom_call_target="tpu_custom_call" | custom-call | tf_op jit(solution)/shard_map/pallas_call | solution.py:525
  86.6 1.4 %copy.8 = f32[1,32,256]{2,1,0:T(8,128)} copy(f32[1,32,256]{2,1,0:T(8,128)} %bitcast.1) | data formatting | bytes 65536
  88.0 1.7 %copy.9 = f32[256,256]{1,0:T(8,128)} copy(f32[256,256]{1,0:T(8,128)} %get-tuple-element.9) | data formatting | bytes 524288

commit v3 on v2

--- a/solution.py
+++ b/solution.py
@@ -17,8 +17,11 @@
 ROWS = 16
 SHARE = BS // NODES
 COLS = 256
-PIECE = COLS // NODES
+PIECE = COLS // NODES // 2
 NCH = 8
+PARTS = 4
+SIDE = 4
+HEIGHT = ROWS // 2
 HALF = NVEC // NCH
 CH = 2 * HALF
 
@@ -61,10 +64,10 @@
 
 
 def kernel(inv, coup, vec, mom, gram,
-           a_f, c_f, v_f, vt, vo, ath, atl, ch, cl, cth, ctl, mth, mtl, nth, ntl, pth, ptl, qth, qtl,
+           a_f, c_f, vt, vo, ath, atl, ch, cl, cth, ctl, mth, mtl, nth, ntl, pth, ptl, qth, qtl,
            snd, rcv, qf, yb, dd, fr, cf, fo, fs, us, uo, es, eo, br, xe, xs,
-           xt, xa, xr, ga, gr, pa, pr, qa, go,
-           in_sem, pss, prs, css, crs, xss, xrs, gss, grs, hss, hrs, qss, qrs):
+           xt, xa, xr, ga, gr, pa, pr, qa, go, fb, fp,
+           in_sem, oss, ors, pss, prs, css, crs, xss, xrs, gss, grs, hss, hrs, qss, qrs, plane_sem):
     k = lax.axis_index("row")
     n = lax.axis_index("node")
     core = lax.rem(k, 2)
@@ -76,20 +79,31 @@
         pltpu.make_async_copy(inv.at[0, 0, 0], a_f.at[0], in_sem.at[0]),
         pltpu.make_async_copy(inv.at[0, 0, 1], a_f.at[1], in_sem.at[1]),
         pltpu.make_async_copy(coup.at[0], c_f, in_sem.at[2]),
-        pltpu.make_async_copy(vec.at[0], v_f, in_sem.at[3]),
+        pltpu.make_async_copy(vec, vt, in_sem.at[3]),
     ]
     for load in loads:
         load.start()
 
     barrier = pltpu.get_barrier_semaphore()
 
-    @pl.loop(1, NODES)
-    def _(d):
-        pl.semaphore_signal(barrier, inc=1, device_id={"node": lax.rem(n + d, NODES)}, device_id_type=MESH)
-
-    @pl.loop(1, ROWS)
-    def _(d):
-        pl.semaphore_signal(barrier, inc=1, device_id={"row": lax.rem(k + d, ROWS)}, device_id_type=MESH)
+    def plane_signal(sem):
+        across = lax.rem(n, SIDE)
+        base = n - across
+        for d in range(1, SIDE):
+            pl.semaphore_signal(sem, inc=1, device_id={"node": base + lax.rem(across + d, SIDE)}, device_id_type=MESH)
+            pl.semaphore_signal(sem, inc=1, device_id={"node": lax.rem(n + d * SIDE, NODES)}, device_id_type=MESH)
+
+    plane_signal(barrier)
+
+    pl.semaphore_signal(barrier, inc=1, device_id={"row": partner}, device_id_type=MESH)
+
+    @pl.when(z > 0)
+    def _():
+        pl.semaphore_signal(barrier, inc=1, device_id={"row": k - 2}, device_id_type=MESH)
+
+    @pl.when(z < top)
+    def _():
+        pl.semaphore_signal(barrier, inc=1, device_id={"row": k + 2}, device_id_type=MESH)
 
     for part in range(2):
         loads[part].wait()
@@ -109,20 +123,17 @@
         cth[:, rows] = high
         ctl[:, rows] = low
     loads[3].wait()
-    v_t = v_f[...].T
-    for q in range(NCH):
-        vt[q] = v_t[q * HALF:(q + 1) * HALF]
 
     def block_loop(count):
         def wrap(step):
             @pl.loop(0, count)
             def _(b):
-                step(pl.ds(pl.multiple_of(b * (BS // count), BS // count), BS // count))
+                step(b, pl.ds(pl.multiple_of(b * (BS // count), BS // count), BS // count))
         return wrap
 
     def forward_operator(keep):
         @block_loop(4)
-        def _(rows):
+        def _(b, rows):
             for part in range(2):
                 cols = slice(part * BS, (part + 1) * BS)
                 value = dot3(ath[rows, cols], atl[rows, cols], ch[...], cl[...])
@@ -131,10 +142,14 @@
                 high, low = split(value)
                 mth[rows, cols] = high
                 mtl[rows, cols] = low
+            if keep:
+                @pl.when((z > 0) & (z < top))
+                def _():
+                    operator(b).start()
 
     def backward_operator(keep):
         @block_loop(4)
-        def _(rows):
+        def _(b, rows):
             for part in range(2):
                 cols = slice(part * BS, (part + 1) * BS)
                 value = dot3(cth[rows, :], ctl[rows, :], ath[:, cols], atl[:, cols])
@@ -143,12 +158,15 @@
                 high, low = split(value)
                 nth[rows, cols] = high
                 ntl[rows, cols] = low
+            if keep:
+                operator(b).start()
 
     def compose(left, rows, wh, wl):
         x = jnp.concatenate([left[rows, :BS], left[rows, BS:]], axis=0)
-        out = complex_apply(x, wh, wl)
-        half = out.shape[0] // 2
-        return out[:half], out[half:]
+        high, low = split(x)
+        y = dot3(high, low, wh[...], wl[...])
+        half = y.shape[0] // 2
+        return y[:half, :BS] - y[half:, BS:], y[:half, BS:] + y[half:, :BS]
 
     def store_split(rows, parts, wh, wl):
         for part, value in enumerate(parts):
@@ -176,7 +194,13 @@
     term = chunk_copy(4, es, eo, partner)
     backward = chunk_copy(5, xe, br, k - 2)
     solved = chunk_copy(6, xe, xs, partner)
-    operator = whole_copy(0, snd, rcv)
+
+    def operator(b):
+        rows = pl.ds(pl.multiple_of(b * (BS // PARTS), BS // PARTS), BS // PARTS)
+        return pltpu.make_async_remote_copy(
+            src_ref=snd.at[rows, :], dst_ref=rcv.at[rows, :], send_sem=oss.at[b], recv_sem=ors.at[b],
+            device_id={"row": partner}, device_id_type=MESH)
+
     probe = whole_copy(1, vt, vo)
     second = whole_copy(2, qf, qf)
 
@@ -189,7 +213,9 @@
         return jnp.concatenate([carry[:HALF] + v, carry[HALF:]], axis=0)
 
     def enter():
-        pl.semaphore_wait(barrier, NODES + ROWS - 2)
+        ends = (z == 0).astype(jnp.int32) + (z == top).astype(jnp.int32)
+        pl.semaphore_wait(barrier, 2 * (SIDE - 1) + 3 - ends)
+        plane_signal(plane_sem)
 
     def real_rows(v):
         return jnp.concatenate([v, jnp.zeros_like(v)], axis=0)
@@ -208,38 +234,35 @@
 
     @pl.when(core == 0)
     def _():
-        forward_operator(True)
         enter()
         probe.start()
-
-        @pl.when((z > 0) & (z < top))
-        def _():
-            operator.start()
+        forward_operator(True)
 
         @pl.when(z == 0)
         def _():
             even_forward(True)
 
         backward_operator(False)
-        operator.wait_recv()
         probe.wait_recv()
 
         @pl.when(z < top)
         def _():
-            @block_loop(8)
-            def _(rows):
+            @block_loop(PARTS)
+            def _(b, rows):
+                operator(b).wait_recv()
                 re, im = compose(rcv, rows, nth, ntl)
                 qf[rows, :BS] = re
                 qf[rows, BS:] = im
 
         @pl.when(z == top)
         def _():
-            @block_loop(8)
-            def _(rows):
+            @block_loop(PARTS)
+            def _(b, rows):
+                operator(b).wait_recv()
                 store_split(rows, compose(rcv, rows, nth, ntl), pth, ptl)
 
-            @block_loop(8)
-            def _(rows):
+            @block_loop(PARTS)
+            def _(b, rows):
                 re, im = compose(snd, rows, pth, ptl)
                 qf[rows, :BS] = re + (ath[rows, :BS].astype(F32) + atl[rows, :BS].astype(F32))
                 qf[rows, BS:] = im + (ath[rows, BS:].astype(F32) + atl[rows, BS:].astype(F32))
@@ -287,9 +310,9 @@
     def _():
         @pl.when(z == 0)
         def _():
-            forward_operator(False)
             enter()
             probe.start()
+            forward_operator(False)
 
             @chunks
             def _(q):
@@ -306,28 +329,26 @@
                 upper(q).start()
 
             backward_operator(True)
-            operator.start()
             probe.wait_recv()
 
         @pl.when((z > 0) & (z < top))
         def _():
-            backward_operator(True)
             enter()
-            operator.start()
             probe.start()
             forward_operator(False)
 
-            @chunks
-            def _(q):
-                dd[q] = complex_apply(real_rows(vt[q]), mth, mtl)
-
-            operator.wait_recv()
-
-            @block_loop(8)
-            def _(rows):
+            dd[...] = apply_all(jnp.concatenate([vt[...], jnp.zeros_like(vt)], axis=1), mth, mtl)
+
+            @block_loop(PARTS)
+            def _(b, rows):
+                operator(b).wait_recv()
                 store_split(rows, compose(rcv, rows, mth, mtl), pth, ptl)
 
             probe.wait_recv()
+
+            @pl.when(z > 1)
+            def _():
+                backward_operator(True)
 
             @chunks
             def _(q):
@@ -336,24 +357,29 @@
                 fs[q] = dd[q] + complex_apply(shifted_by(fr[q], vo[q]), pth, ptl)
                 forward(q).start()
 
+            @pl.when(z == 1)
+            def _():
+                backward_operator(True)
+
             odd_upper()
 
         def take_second(wh, wl):
             second.wait_recv()
 
             @block_loop(8)
-            def _(rows):
+            def _(b, rows):
                 store_split(rows, (qf[rows, :BS], qf[rows, BS:]), wh, wl)
 
         @pl.when(z == top)
         def _():
-            @block_loop(8)
-            def _(rows):
+            enter()
+            probe.start()
+
+            @block_loop(PARTS)
+            def _(b, rows):
                 snd[rows, :] = ath[rows, :].astype(F32) + atl[rows, :].astype(F32)
-
-            enter()
-            operator.start()
-            probe.start()
+                operator(b).start()
+
             probe.wait_recv()
             take_second(pth, ptl)
 
@@ -390,6 +416,8 @@
                 solved(q).start()
 
             xs[...] = us[...] + apply_all(br[...], nth, ntl)
+
+    pl.semaphore_wait(plane_sem, 2 * (SIDE - 1))
 
     for q in range(NCH):
         x = xs[q]
@@ -450,8 +478,13 @@
     f = jnp.concatenate(parts, axis=1)
     mom[...] = f
 
-    fh, fl = split(f)
-    th, tl = split(f.T)
+    fb[...] = f
+    other = whole_copy(3, fb, fp)
+    other.start()
+    other.wait_recv()
+    pair = jnp.concatenate([f, fp[...]], axis=0)
+    fh, fl = split(pair)
+    th, tl = split(jnp.where(core == 0, pair[:, :COLS // 2], pair[:, COLS // 2:]).T)
     product = dot3(th, tl, fh, fl)
     for j in range(NODES):
         ga[j] = product[j * PIECE:(j + 1) * PIECE]
@@ -462,25 +495,69 @@
     for j in range(1, NODES):
         total = total + gr[j]
     pa[...] = total
-    pr[k] = total
-    finish, sent_p = spread("row", ROWS, k, pa, pr, hss, hrs, False)
-    finish()
+    pr[z] = total
+
+    def column(d):
+        level = lax.rem(z + d, HEIGHT)
+        return pltpu.make_async_remote_copy(
+            src_ref=pa, dst_ref=pr.at[z], send_sem=hss.at[d], recv_sem=hrs.at[z],
+            device_id={"row": 2 * level + core}, device_id_type=MESH)
+
+    def column_arrival(d):
+        level = lax.rem(z + d, HEIGHT)
+        return pltpu.make_async_remote_copy(
+            src_ref=pa, dst_ref=pr.at[level], send_sem=hss.at[d], recv_sem=hrs.at[level],
+            device_id={"row": 2 * level + core}, device_id_type=MESH)
+
+    @pl.loop(1, HEIGHT)
+    def _(d):
+        column(d).start()
+
+    @pl.loop(1, HEIGHT)
+    def _(d):
+        column_arrival(d).wait_recv()
+
     total = pr[0]
-    for j in range(1, ROWS):
+    for j in range(1, HEIGHT):
         total = total + pr[j]
     total = total * (NODES / (ROWS * BS))
     qa[...] = total
-    go[n] = total
-    finish, sent_q = spread("node", NODES, n, qa, go, qss, qrs, False)
-    finish()
-    for j in range(NODES):
-        gram[j * PIECE:(j + 1) * PIECE, :] = go[j]
+    go[core, n] = total
+
+    def result(side, d):
+        return pltpu.make_async_remote_copy(
+            src_ref=qa, dst_ref=go.at[core, n], send_sem=qss.at[side, d], recv_sem=qrs.at[core, n],
+            device_id={"node": lax.rem(n + d, NODES), "row": partner if side else k}, device_id_type=MESH)
+
+    def result_arrival(side, d):
+        peer = lax.rem(n + d, NODES)
+        source = 1 - core if side else core
+        return pltpu.make_async_remote_copy(
+            src_ref=qa, dst_ref=go.at[source, peer], send_sem=qss.at[side, d], recv_sem=qrs.at[source, peer],
+            device_id={"node": peer, "row": partner if side else k}, device_id_type=MESH)
+
+    def results(step):
+        @pl.loop(1, NODES)
+        def _(d):
+            step(0, d)
+            step(1, d)
+
+        step(1, 0)
+
+    results(lambda side, d: result(side, d).start())
+    results(lambda side, d: result_arrival(side, d).wait_recv())
+    for c in range(2):
+        for j in range(NODES):
+            at = c * (COLS // 2) + j * PIECE
+            gram[at:at + PIECE, :] = go[c, j]
 
     probe.wait_send()
 
     @pl.when((core == 1) | ((z > 0) & (z < top)))
     def _():
-        operator.wait_send()
+        @pl.loop(0, PARTS)
+        def _(b):
+            operator(b).wait_send()
 
     @pl.when(core == 0)
     def _():
@@ -513,8 +590,13 @@
 
     sent_x()
     sent_g()
-    sent_p()
-    sent_q()
+    other.wait_send()
+
+    @pl.loop(1, HEIGHT)
+    def _(d):
+        column(d).wait_send()
+
+    results(lambda side, d: result(side, d).wait_send())
 
 
 def shards(inv_factors, coupling, vectors):
@@ -533,7 +615,6 @@
         scratch_shapes=[
             pltpu.VMEM((2, BS, BS), F32),
             pltpu.VMEM((BS, BS), F32),
-            pltpu.VMEM((BS, NVEC), F32),
             pltpu.VMEM((NCH, HALF, BS), F32),
             pltpu.VMEM((NCH, HALF, BS), F32),
         ]
@@ -549,17 +630,22 @@
             pltpu.VMEM((NODES, PIECE, COLS), F32),
             pltpu.VMEM((NODES, PIECE, COLS), F32),
             pltpu.VMEM((PIECE, COLS), F32),
-            pltpu.VMEM((ROWS, PIECE, COLS), F32),
+            pltpu.VMEM((HEIGHT, PIECE, COLS), F32),
             pltpu.VMEM((PIECE, COLS), F32),
-            pltpu.VMEM((NODES, PIECE, COLS), F32),
+            pltpu.VMEM((2, NODES, PIECE, COLS), F32),
+            pltpu.VMEM((SHARE, COLS), F32),
+            pltpu.VMEM((SHARE, COLS), F32),
         ]
         + [pltpu.SemaphoreType.DMA((4,))]
-        + [pltpu.SemaphoreType.DMA((3,))] * 2
+        + [pltpu.SemaphoreType.DMA((PARTS,))] * 2
+        + [pltpu.SemaphoreType.DMA((4,))] * 2
         + [pltpu.SemaphoreType.DMA((7, NCH))] * 2
-        + [pltpu.SemaphoreType.DMA((16,))] * 8,
+        + [pltpu.SemaphoreType.DMA((16,))] * 6
+        + [pltpu.SemaphoreType.DMA((2, 16))] * 2
+        + [pltpu.SemaphoreType.REGULAR],
         compiler_params=pltpu.CompilerParams(
             collective_id=0, has_side_effects=True, vmem_limit_bytes=56 * 1024 * 1024),
-    )(inv_factors, coupling, vectors)
+    )(inv_factors, coupling, jnp.swapaxes(vectors, 1, 2).reshape(NCH, HALF, BS))
     return moments[None], gram
 
 

time: 90.5 us -> 81.5 us (0.901)
  Pallas kernels: 84.2 us -> 77.7 us
  local copies, waits for them, and re-layouts: 4.78 us -> 3.04 us
    pallas_call x1, Pallas kernels: 84.2 us -> 77.7 us  [shards(): pl.pallas_call(kernel, out_shape=(jax.ShapeDtypeStruct((SHARE, COLS), F32...]
    unnamed x3 -> x2, local copies, waits for them, and re-layouts: 4.78 us -> 3.04 us
where the time goes in v3:
time: 81.5 us; the launch traced here: 81.4 us
  Pallas kernels  77.7 us (95%)
  local copies, waits for them, and re-layouts  3.04 us (4%)
    pallas_call x1, Pallas kernels, shards(): pl.pallas_call(kernel, out_shape=(jax.ShapeDtypeStruct((SHARE, COLS), F32...  77.7 us
    unnamed x2, local copies, waits for them, and re-layouts  3.04 us

profile of v3, /device:TPU:33, one launch (start us, length us, event | category | flops | bytes accessed | tf_op | source)
XLA Modules:
  0.0 81.4 jit_solution(14908750629655922755)
XLA Ops:
  0.6 77.7 %shard_map.50 = (f32[32,256]{1,0:T(8,128)}, f32[256,256]{1,0:T(8,128)}) custom-call(f32[1,1,2,512,512]{4,3,2,1,0:T(8,128)} %inv.1, f32[1,512,512]{2,1,0:T(8,128)} %coup.1, f32[8,8,512]{2,1,0:T(8,128)} %bitcast.4), custom_call_target="tpu_custom_call" | custom-call | tf_op jit(solution)/shard_map/pallas_call | solution.py:607
  78.3 1.4 %copy.7 = f32[1,32,256]{2,1,0:T(8,128)} copy(f32[1,32,256]{2,1,0:T(8,128)} %bitcast.5) | data formatting | bytes 65536
  79.7 1.7 %copy.8 = f32[256,256]{1,0:T(8,128)} copy(f32[256,256]{1,0:T(8,128)} %get-tuple-element.9) | data formatting | bytes 524288

commit v4 on v3

--- a/solution.py
+++ b/solution.py
@@ -63,11 +63,11 @@
     return complex_apply(x.reshape(NCH * CH, BS), wh, wl, NCH).reshape(NCH, CH, BS)
 
 
-def kernel(inv, coup, vec, mom, gram,
-           a_f, c_f, vt, vo, ath, atl, ch, cl, cth, ctl, mth, mtl, nth, ntl, pth, ptl, qth, qtl,
+def kernel(inv, coup, vt, mom, gram,
+           vo, ath, atl, ch, cl, cth, ctl, mth, mtl, nth, ntl, pth, ptl, qth, qtl,
            snd, rcv, qf, yb, dd, fr, cf, fo, fs, us, uo, es, eo, br, xe, xs,
            xt, xa, xr, ga, gr, pa, pr, qa, go, fb, fp,
-           in_sem, oss, ors, pss, prs, css, crs, xss, xrs, gss, grs, hss, hrs, qss, qrs, plane_sem):
+           oss, ors, pss, prs, css, crs, xss, xrs, gss, grs, hss, hrs, qss, qrs, plane_sem):
     k = lax.axis_index("row")
     n = lax.axis_index("node")
     core = lax.rem(k, 2)
@@ -75,15 +75,6 @@
     top = ROWS // 2 - 1
     partner = k + 1 - 2 * core
 
-    loads = [
-        pltpu.make_async_copy(inv.at[0, 0, 0], a_f.at[0], in_sem.at[0]),
-        pltpu.make_async_copy(inv.at[0, 0, 1], a_f.at[1], in_sem.at[1]),
-        pltpu.make_async_copy(coup.at[0], c_f, in_sem.at[2]),
-        pltpu.make_async_copy(vec, vt, in_sem.at[3]),
-    ]
-    for load in loads:
-        load.start()
-
     barrier = pltpu.get_barrier_semaphore()
 
     def plane_signal(sem):
@@ -106,23 +97,20 @@
         pl.semaphore_signal(barrier, inc=1, device_id={"row": k + 2}, device_id_type=MESH)
 
     for part in range(2):
-        loads[part].wait()
         for b in range(4):
-            high, low = split(a_f[part, b * 128:(b + 1) * 128, :].T)
+            high, low = split(inv[0, 0, part, b * 128:(b + 1) * 128, :].T)
             at = part * BS + b * 128
             ath[:, at:at + 128] = high
             atl[:, at:at + 128] = low
-    loads[2].wait()
     for b in range(4):
         rows = slice(b * 128, (b + 1) * 128)
-        block = c_f[rows, :]
+        block = coup[0, rows, :]
         high, low = split(block)
         ch[rows, :] = high
         cl[rows, :] = low
         high, low = split(block.T)
         cth[:, rows] = high
         ctl[:, rows] = low
-    loads[3].wait()
 
     def block_loop(count):
         def wrap(step):
@@ -143,6 +131,11 @@
                 mth[rows, cols] = high
                 mtl[rows, cols] = low
             if keep:
+                @pl.when(b == 0)
+                def _():
+                    enter()
+                    probe.start()
+
                 @pl.when((z > 0) & (z < top))
                 def _():
                     operator(b).start()
@@ -234,8 +227,6 @@
 
     @pl.when(core == 0)
     def _():
-        enter()
-        probe.start()
         forward_operator(True)
 
         @pl.when(z == 0)
@@ -298,21 +289,16 @@
         @chunks
         def _(q):
             inner(q).wait_recv()
-            yb[q] = shifted_by(fo[q], vt[q])
-
-        us[...] = apply_all(yb[...], ath, atl)
-
-        @chunks
-        def _(q):
+            us[q] = complex_apply(shifted_by(fo[q], vt[q]), ath, atl)
             upper(q).start()
 
     @pl.when(core == 1)
     def _():
         @pl.when(z == 0)
         def _():
+            forward_operator(False)
             enter()
             probe.start()
-            forward_operator(False)
 
             @chunks
             def _(q):
@@ -333,10 +319,9 @@
 
         @pl.when((z > 0) & (z < top))
         def _():
+            forward_operator(False)
             enter()
             probe.start()
-            forward_operator(False)
-
             dd[...] = apply_all(jnp.concatenate([vt[...], jnp.zeros_like(vt)], axis=1), mth, mtl)
 
             @block_loop(PARTS)
@@ -610,12 +595,9 @@
             jax.ShapeDtypeStruct((SHARE, COLS), F32),
             jax.ShapeDtypeStruct((COLS, COLS), F32),
         ),
-        in_specs=[pl.BlockSpec(memory_space=pl.ANY)] * 3,
+        in_specs=[pl.BlockSpec(memory_space=pltpu.VMEM)] * 3,
         out_specs=[pl.BlockSpec(memory_space=pltpu.VMEM)] * 2,
         scratch_shapes=[
-            pltpu.VMEM((2, BS, BS), F32),
-            pltpu.VMEM((BS, BS), F32),
-            pltpu.VMEM((NCH, HALF, BS), F32),
             pltpu.VMEM((NCH, HALF, BS), F32),
         ]
         + [whole_part] * 2
@@ -636,7 +618,6 @@
             pltpu.VMEM((SHARE, COLS), F32),
             pltpu.VMEM((SHARE, COLS), F32),
         ]
-        + [pltpu.SemaphoreType.DMA((4,))]
         + [pltpu.SemaphoreType.DMA((PARTS,))] * 2
         + [pltpu.SemaphoreType.DMA((4,))] * 2
         + [pltpu.SemaphoreType.DMA((7, NCH))] * 2
@@ -644,7 +625,7 @@
         + [pltpu.SemaphoreType.DMA((2, 16))] * 2
         + [pltpu.SemaphoreType.REGULAR],
         compiler_params=pltpu.CompilerParams(
-            collective_id=0, has_side_effects=True, vmem_limit_bytes=56 * 1024 * 1024),
+            collective_id=0, has_side_effects=True, vmem_limit_bytes=40 * 1024 * 1024),
     )(inv_factors, coupling, jnp.swapaxes(vectors, 1, 2).reshape(NCH, HALF, BS))
     return moments[None], gram
 

time: 81.5 us -> 80.3 us (0.985)
  Pallas kernels: 77.7 us -> 74.5 us
  local copies, waits for them, and re-layouts: 3.04 us -> 5.03 us
    pallas_call x1, Pallas kernels: 77.7 us -> 74.5 us  [shards(): pl.pallas_call(kernel, out_shape=(jax.ShapeDtypeStruct((SHARE, COLS), F32...]
    unnamed x2 -> x8, local copies, waits for them, and re-layouts: 3.04 us -> 5.03 us
where the time goes in v4:
time: 80.3 us; the launch traced here: 80.1 us
  Pallas kernels  74.5 us (93%)
  local copies, waits for them, and re-layouts  5.03 us (6%)
    pallas_call x1, Pallas kernels, shards(): pl.pallas_call(kernel, out_shape=(jax.ShapeDtypeStruct((SHARE, COLS), F32...  74.5 us
    unnamed x8, local copies, waits for them, and re-layouts  5.03 us

profile of v4, /device:TPU:33, one launch (start us, length us, event | category | flops | bytes accessed | tf_op | source)
XLA Modules:
  0.0 80.1 jit_solution(6403559595049389208)
XLA Ops:
  0.6 0.0 copy-start
  0.6 1.6 %copy-done = f32[1,1,2,512,512]{4,3,2,1,0:T(8,128)S(1)} copy-done((f32[1,1,2,512,512]{4,3,2,1,0:T(8,128)S(1)}, f32[1,1,2,512,512]{4,3,2,1,0:T(8,128)}, u32[]{:S(2)}) %copy-start) | copy-done | bytes 2097176
  2.2 0.0 copy-start.1
  2.2 1.2 %copy-done.1 = f32[1,512,512]{2,1,0:T(8,128)S(1)} copy-done((f32[1,512,512]{2,1,0:T(8,128)S(1)}, f32[1,512,512]{2,1,0:T(8,128)}, u32[]{:S(2)}) %copy-start.1) | copy-done | bytes 1048600
  3.4 0.0 copy-start.2
  3.4 0.9 %copy-done.2 = f32[1,512,64]{1,2,0:T(8,128)S(1)} copy-done((f32[1,512,64]{1,2,0:T(8,128)S(1)}, f32[1,512,64]{1,2,0:T(8,128)}, u32[]{:S(2)}) %copy-start.2) | copy-done | bytes 131096
  4.4 74.5 %shard_map.50 = (f32[32,256]{1,0:T(8,128)S(1)}, f32[256,256]{1,0:T(8,128)S(1)}) custom-call(f32[1,1,2,512,512]{4,3,2,1,0:T(8,128)S(1)} %copy-done, f32[1,512,512]{2,1,0:T(8,128)S(1)} %copy-done.1, f32[8,8,512]{2,1,0:T(8,128)S(1)} %bitcast.4), custom_call_target="tpu_custom_call" | custom-call | tf_op jit(solution)/shard_map/pallas_call | solution.py:592
  78.8 0.6 copy.7
  79.4 0.7 copy.8
Async XLA Ops:
  0.6 1.6 %copy-start = (f32[1,1,2,512,512]{4,3,2,1,0:T(8,128)S(1)}, f32[1,1,2,512,512]{4,3,2,1,0:T(8,128)}, u32[]{:S(2)}) copy-start(f32[1,1,2,512,512]{4,3,2,1,0:T(8,128)} %inv.1) | copy-start | bytes 6291460
  2.2 1.2 %copy-start.1 = (f32[1,512,512]{2,1,0:T(8,128)S(1)}, f32[1,512,512]{2,1,0:T(8,128)}, u32[]{:S(2)}) copy-start(f32[1,512,512]{2,1,0:T(8,128)} %coup.1) | copy-start | bytes 3145732
  3.4 0.9 %copy-start.2 = (f32[1,512,64]{1,2,0:T(8,128)S(1)}, f32[1,512,64]{1,2,0:T(8,128)}, u32[]{:S(2)}) copy-start(f32[1,512,64]{1,2,0:T(8,128)} %param.5) | copy-start | bytes 393220

commit v5 on v4

--- a/solution.py
+++ b/solution.py
@@ -108,9 +108,6 @@
         high, low = split(block)
         ch[rows, :] = high
         cl[rows, :] = low
-        high, low = split(block.T)
-        cth[:, rows] = high
-        ctl[:, rows] = low
 
     def block_loop(count):
         def wrap(step):
@@ -141,6 +138,12 @@
                     operator(b).start()
 
     def backward_operator(keep):
+        for b in range(4):
+            rows = slice(b * 128, (b + 1) * 128)
+            high, low = split(coup[0, rows, :].T)
+            cth[:, rows] = high
+            ctl[:, rows] = low
+
         @block_loop(4)
         def _(b, rows):
             for part in range(2):

time: 80.3 us -> 80.7 us (level)
  no operation moved by 1% of the time
where the time goes in v5:
time: 80.7 us; the launch traced here: 80.5 us
  Pallas kernels  74.8 us (93%)
  local copies, waits for them, and re-layouts  5.03 us (6%)
    pallas_call x1, Pallas kernels, shards(): pl.pallas_call(kernel, out_shape=(jax.ShapeDtypeStruct((SHARE, COLS), F32...  74.8 us
    unnamed x8, local copies, waits for them, and re-layouts  5.03 us

profile of v5, /device:TPU:33, one launch (start us, length us, event | category | flops | bytes accessed | tf_op | source)
XLA Modules:
  0.0 80.5 jit_solution(6141234441891259970)
XLA Ops:
  0.6 0.0 copy-start
  0.6 1.6 %copy-done = f32[1,1,2,512,512]{4,3,2,1,0:T(8,128)S(1)} copy-done((f32[1,1,2,512,512]{4,3,2,1,0:T(8,128)S(1)}, f32[1,1,2,512,512]{4,3,2,1,0:T(8,128)}, u32[]{:S(2)}) %copy-start) | copy-done | bytes 2097176
  2.2 0.0 copy-start.1
  2.2 1.2 %copy-done.1 = f32[1,512,512]{2,1,0:T(8,128)S(1)} copy-done((f32[1,512,512]{2,1,0:T(8,128)S(1)}, f32[1,512,512]{2,1,0:T(8,128)}, u32[]{:S(2)}) %copy-start.1) | copy-done | bytes 1048600
  3.4 0.0 copy-start.2
  3.4 0.9 %copy-done.2 = f32[1,512,64]{1,2,0:T(8,128)S(1)} copy-done((f32[1,512,64]{1,2,0:T(8,128)S(1)}, f32[1,512,64]{1,2,0:T(8,128)}, u32[]{:S(2)}) %copy-start.2) | copy-done | bytes 131096
  4.4 74.8 %shard_map.50 = (f32[32,256]{1,0:T(8,128)S(1)}, f32[256,256]{1,0:T(8,128)S(1)}) custom-call(f32[1,1,2,512,512]{4,3,2,1,0:T(8,128)S(1)} %copy-done, f32[1,512,512]{2,1,0:T(8,128)S(1)} %copy-done.1, f32[8,8,512]{2,1,0:T(8,128)S(1)} %bitcast.4), custom_call_target="tpu_custom_call" | custom-call | tf_op jit(solution)/shard_map/pallas_call | solution.py:595
  79.2 0.6 copy.7
  79.8 0.7 copy.8
Async XLA Ops:
  0.6 1.6 %copy-start = (f32[1,1,2,512,512]{4,3,2,1,0:T(8,128)S(1)}, f32[1,1,2,512,512]{4,3,2,1,0:T(8,128)}, u32[]{:S(2)}) copy-start(f32[1,1,2,512,512]{4,3,2,1,0:T(8,128)} %inv.1) | copy-start | bytes 6291460
  2.2 1.2 %copy-start.1 = (f32[1,512,512]{2,1,0:T(8,128)S(1)}, f32[1,512,512]{2,1,0:T(8,128)}, u32[]{:S(2)}) copy-start(f32[1,512,512]{2,1,0:T(8,128)} %coup.1) | copy-start | bytes 3145732
  3.4 0.9 %copy-start.2 = (f32[1,512,64]{1,2,0:T(8,128)S(1)}, f32[1,512,64]{1,2,0:T(8,128)}, u32[]{:S(2)}) copy-start(f32[1,512,64]{1,2,0:T(8,128)} %param.5) | copy-start | bytes 393220
